TPU v7x, 32 devices: a whole 2x2x4 slice. The times are simulated.
32 devices in a mesh: shots: 2 (over y), rx: 4 (over z), ta: 2 (over x), af: 2 (over core).
Axes of the slice: x: 2, y: 2, z: 4, core: 2. Of those that a mesh axis runs over, the one named last changes fastest.
Arguments:
- traces: bfloat16 [4096, 512], P(('shots', 'rx'), ('ta', 'af')), parts along dimension 0, may hold values from -6 to 6
- slopes: int32 [512], replicated, may hold values from 0 to 1023
- offsets: int32 [4096], P('shots'), parts along dimension 0, may hold values from 1 to 4095
- live: int32 [4096], P('shots'), parts along dimension 0, may hold values 0 or 1
Outputs:
- stack: float32 [1024, 512], P(('shots', 'rx'), ('ta', 'af')), parts along dimension 0
- coherence: float32 [1024, 512], P(('shots', 'rx'), ('ta', 'af')), parts along dimension 0
- peak_values: float32 [1024], P(('shots', 'rx')), parts along dimension 0
There are 2 independent parts, one for each index of `shots`. A program takes and returns all parts, laid end to end along the dimension named above; an argument that names none is the same for every part. Nothing has to cross between parts.
Inputs may be any that keep to these rules, and one draw needn't show every extreme that they name: delays are below 64: (slopes * offsets) // 65536 < 64.
All inputs are finite; a program needn't handle non-finite values.
Results may differ from a plain program's by a relative error of at most 0.0003.
Values may be sent and summed in bfloat16 or wider, within the bound.
A program may use at most 64 MiB of HBM per device.

v0:
```python
import jax
import jax.numpy as jnp
from jax import lax
from jax.sharding import PartitionSpec as P

SPAN = 64
WIN = 16


def passed_along(value, axis, steps):
    count = lax.axis_size(axis)
    leading, last = (max(0, -steps), min(count, count - steps))
    return lax.ppermute(value, axis, [(source, source + steps) for source in range(leading, last)])


def hankel(samples, delay_span, block_len):
    row_total, length = samples.shape
    repeated = jnp.tile(samples, (1, delay_span))
    repeated = jnp.pad(repeated, ((0, 0), (0, delay_span)))
    return repeated.reshape(row_total, delay_span, length + 1)[:, :, :block_len]


def build_lagged(samples, delay_span, block_len):
    squared = (samples.astype(jnp.float32) ** 2).astype(jnp.bfloat16)
    return (hankel(samples, delay_span, block_len), hankel(squared, delay_span, block_len))


def project_lags(slope_rows, offset_rows, lagged_x, lagged_s, delay_span):
    delays = slope_rows[:, None] * offset_rows[None, :] // 65536
    lags = jnp.arange(delay_span, dtype=jnp.int32)
    onehot = (delays[:, :, None] == lags[None, None, :]).astype(jnp.bfloat16)
    stacked = jnp.einsum("prk,rkt->pt", onehot, lagged_x, preferred_element_type=jnp.float32)
    energy = jnp.einsum("prk,rkt->pt", onehot, lagged_s, preferred_element_type=jnp.float32)
    return jnp.concatenate([stacked, energy], axis=1)


def on_device(traces, slopes, offsets, live):
    receiver_group = lax.axis_index("rx")
    local_rows, block_len = traces.shape
    delay_span = SPAN
    window = WIN
    live_gain = lax.dynamic_slice_in_dim(live, receiver_group * local_rows, local_rows).astype(
        jnp.bfloat16
    )
    offset_local = lax.dynamic_slice_in_dim(offsets, receiver_group * local_rows, local_rows)
    weighted = traces * live_gain[:, None]
    arriving = passed_along(weighted[:, :delay_span], ("ta", "af"), -1)
    extended = jnp.concatenate([weighted, arriving], axis=1)
    local_x, local_s = build_lagged(extended, delay_span, block_len)
    summed = lax.psum_scatter(
        project_lags(slopes, offset_local, local_x, local_s, delay_span),
        "rx",
        scatter_dimension=0,
        tiled=True,
    )
    stack = summed[:, :block_len]
    energy = summed[:, block_len:]
    following = passed_along((stack[:, :window], energy[:, :window]), ("ta", "af"), -1)
    long_stack = jnp.concatenate([stack, following[0]], axis=1)
    long_energy = jnp.concatenate([energy, following[1]], axis=1)
    power_sum = jnp.zeros_like(stack)
    energy_sum = jnp.zeros_like(energy)
    for lag_index in range(window):
        power_sum = power_sum + long_stack[:, lag_index : lag_index + block_len] ** 2
        energy_sum = energy_sum + long_energy[:, lag_index : lag_index + block_len]
    coherence = power_sum / jnp.maximum(energy_sum, 1.0)
    peak_values = lax.pmax(jnp.max(coherence, axis=1), ("ta", "af"))
    return (stack, coherence, peak_values)


def solution(mesh):
    placed = (P(("shots", "rx"), ("ta", "af")), P(), P("shots"), P("shots"))
    return jax.shard_map(
        on_device,
        mesh=mesh,
        in_specs=placed,
        out_specs=(
            P(("shots", "rx"), ("ta", "af")),
            P(("shots", "rx"), ("ta", "af")),
            P(("shots", "rx")),
        ),
        check_vma=False,
    )
```

profile of v0, /device:TPU:0, one launch (start us, length us, event | category | flops | bytes accessed | tf_op | source)
XLA Modules:
  0.0 147.2 jit_solution(1106759283798716717)
XLA Ops:
  7.2 0.0 reduce-scatter.2.cloned.1.call-start
  7.2 1.0 copy.15
  8.2 0.8 dynamic-slice_convert_fusion
  9.0 1.3 collective-permute-start
  10.3 0.8 dynamic_slice.6
  11.1 1.4 add_select_fusion
  12.5 0.0 collective-permute-done
  12.5 6.1 %tile.8 = bf16[512,64,192]{0,2,1:T(8,128)(2,1)} broadcast(bf16[512,192]{0,1:T(8,128)(2,1)S(1)} %pad_maximum_fusion.1), dimensions={0,2} | broadcast | bytes 12779520 | tf_op jit(solution)/shard_map/tile | solution.py:18
  18.6 10.6 %pad.7 = bf16[512,12352]{0,1:T(8,128)(2,1)} pad(bf16[512,12288]{0,1:T(8,128)(2,1)} %bitcast.11, bf16[]{:T(256)} %constant.29.clone.1), padding=0_0x0_64 | pad | bytes 25231362 | tf_op jit(solution)/shard_map/jit(_pad)/pad | solution.py:19
  29.1 12.8 %reshape.79 = bf16[512,64,193]{0,2,1:T(8,128)(2,1)} reshape(bf16[512,12352]{0,1:T(8,128)(2,1)} %pad.7) | data formatting | bytes 25296896 | tf_op jit(solution)/shard_map/reshape | solution.py:20
  41.9 6.0 %tile.20 = bf16[512,64,192]{0,2,1:T(8,128)(2,1)} broadcast(bf16[512,192]{0,1:T(8,128)(2,1)S(1)} %multiply_convert_fusion), dimensions={0,2} | broadcast | bytes 12779520 | tf_op jit(solution)/shard_map/tile | solution.py:18
  48.0 10.5 %pad.8 = bf16[512,12352]{0,1:T(8,128)(2,1)} pad(bf16[512,12288]{0,1:T(8,128)(2,1)} %bitcast.10, bf16[]{:T(256)} %constant.29.clone.1), padding=0_0x0_64 | pad | bytes 25231362 | tf_op jit(solution)/shard_map/jit(_pad)/pad | solution.py:19
  58.5 12.8 %reshape.80 = bf16[512,64,193]{0,2,1:T(8,128)(2,1)} reshape(bf16[512,12352]{0,1:T(8,128)(2,1)} %pad.8) | data formatting | bytes 25296896 | tf_op jit(solution)/shard_map/reshape | solution.py:20
  71.3 0.0 copy-start
  71.3 14.7 %fusion.6 = f32[512,128]{0,1:T(8,128)S(1)} fusion(bf16[512,64,193]{0,2,1:T(8,128)(2,1)} %reshape.79, s32[512,512]{1,0:T(8,128)S(1)} %add_select_fusion), kind=kOutput, calls=%fused_computation.14 | convolution fusion | flops 4311744512 | bytes 9699328 | tf_op jit(solution)/shard_map/prk,rkt->pt/dot_general | solution.py:32
  86.0 0.0 copy-done
  86.0 12.9 %fusion.9 = f32[512,128]{0,1:T(8,128)S(1)} fusion(bf16[512,64,193]{0,2,1:T(8,128)(2,1)S(1)} %copy-done, s32[512,512]{1,0:T(8,128)S(1)} %add_select_fusion), kind=kOutput, calls=%fused_computation.15 | convolution fusion | flops 4311744512 | bytes 9699328 | tf_op jit(solution)/shard_map/prk,rkt->pt/dot_general | solution.py:33
  98.8 0.8 pad_maximum_fusion
  99.7 0.0 reduce-scatter.2.cloned.1.call-update
  99.7 25.5 %reduce-scatter.2.cloned.1.call-done = f32[128,256]{0,1:T(8,128)} async-done(((f32[512,256]{0,1:T(8,128)}), f32[128,256]{0,1:T(8,128)}) %reduce-scatter.2.cloned.1.call-update) | async-done | bytes 131088 | tf_op jit(solution)/shard_map/reduce_scatter | solution.py:50
  125.2 0.7 fusion.94
  125.9 1.3 collective-permute-start.1
  127.2 1.3 collective-permute-start.2
  128.5 0.9 fusion.95
  129.4 0.7 copy.16
  130.1 0.0 collective-permute-done.1
  130.1 0.8 collective-permute-done.2
  130.9 0.2 fusion.92
  131.1 8.6 %pmax.7 = f32[128]{0:T(128)} all-reduce(f32[128]{0:T(128)S(1)} %get-tuple-element.12), channel_id=1, replica_groups=mesh['shots'=2,'rx'=4,'ta'=2,'af'=2] {'ta','af'}, use_global_device_ids=true, to_apply=%region_2.3 | all-reduce | flops 128 | bytes 1024 | tf_op jit(solution)/shard_map/pmax | solution.py:67
  139.6 0.7 copy.17
  (4 shorter events, 0.1 us)
Async XLA Ops:
  7.2 118.0 %reduce-scatter.2.cloned.1.call-start = ((), (), s32[]{:S(2)}) async-start(), calls=%async_computation.1 | async-start | bytes 655360 | tf_op jit(solution)/shard_map/reduce_scatter | solution.py:50
  9.0 3.4 %collective-permute-start = (bf16[512,64]{0,1:T(8,128)(2,1)S(1)}, bf16[512,64]{0,1:T(8,128)(2,1)S(1)}, u32[]{:S(2)}, u32[]{:S(2)}) collective-permute-start(bf16[512,64]{0,1:T(8,128)(2,1)S(1)} %slice.150), channel_id=1, source_target_pairs={{1,0},{2,1},{3,2},{5,4},{6,5},{7,6},{9,8},{10,9},{11,10},{13,12},{... | collective-permute-start | bytes 196616 | tf_op jit(solution)/shard_map/ppermute | solution.py:13
  71.3 14.7 %copy-start = (bf16[512,64,193]{0,2,1:T(8,128)(2,1)S(1)}, bf16[512,64,193]{0,2,1:T(8,128)(2,1)}, u32[]{:S(2)}) copy-start(bf16[512,64,193]{0,2,1:T(8,128)(2,1)} %reshape.80) | copy-start | bytes 37945348
  125.9 4.2 %collective-permute-start.1 = (f32[128,16]{0,1:T(8,128)S(1)}, f32[128,16]{0,1:T(8,128)S(1)}, u32[]{:S(2)}, u32[]{:S(2)}) collective-permute-start(f32[128,16]{0,1:T(8,128)S(1)} %get-tuple-element.14), channel_id=1, source_target_pairs={{1,0},{2,1},{3,2},{5,4},{6,5},{7,6},{9,8},{10,9},{11,10},{13,12},{... | collective-permute-start | bytes 24584 | tf_op jit(solution)/shard_map/ppermute | solution.py:13
  127.2 3.7 %collective-permute-start.2 = (f32[128,16]{0,1:T(8,128)S(1)}, f32[128,16]{0,1:T(8,128)S(1)}, u32[]{:S(2)}, u32[]{:S(2)}) collective-permute-start(f32[128,16]{0,1:T(8,128)S(1)} %get-tuple-element.15), channel_id=1, source_target_pairs={{1,0},{2,1},{3,2},{5,4},{6,5},{7,6},{9,8},{10,9},{11,10},{13,12},{... | collective-permute-start | bytes 24584 | tf_op jit(solution)/shard_map/ppermute | solution.py:13
Sparse Core Ops, SparseCore 0:
  99.8 25.3 reduce-scatter.1
where the time goes:
time: 148 us; the launch traced here: 147 us
  local copies, waits for them, and re-layouts  63.6 us (43%)
  matrix products  27.5 us (19%)
  waiting for transfers between devices  26.3 us (18%)
  between operations  14.1 us (10%)
  blocking collectives  8.56 us (6%)
  starting transfers between devices  3.9 us (3%)
  other arithmetic  3.19 us (2%)
    reshape x2, local copies, waits for them, and re-layouts, hankel(): return repeated.reshape(row_total, delay_span, length + 1)[:, :, :block_len]  25.5 us
    reduce_scatter x1, waiting for transfers between devices, on_device(): lax.psum_scatter(project_lags(slopes, offset_local, local_x, local_s, del...  25.5 us
    pad x2, local copies, waits for them, and re-layouts, hankel(): repeated = jnp.pad(repeated, ((0, 0), (0, delay_span)))  21.1 us
    dot_general x1, matrix products, project_lags(): jnp.einsum('prk,rkt->pt', onehot, lagged_x, preferred_element_type=jnp.fl...  14.7 us
    dot_general x1, matrix products, project_lags(): jnp.einsum('prk,rkt->pt', onehot, lagged_s, preferred_element_type=jnp.fl...  12.9 us
    another operation x2, local copies, waits for them, and re-layouts, hankel(): repeated = jnp.tile(samples, (1, delay_span))  12.1 us
    pmax x1, blocking collectives, on_device(): peak_values = lax.pmax(jnp.max(coherence, axis=1), ('ta', 'af'))  8.56 us
    ppermute x3, starting transfers between devices, passed_along(): lax.ppermute(value, axis, [(source, source + steps) for source in range(l...  3.86 us
  transfers between devices with their start and end apart: 4, of which 2 were waited for; matrix products, arithmetic and copies ran while one was open for 3% of the time, Pallas kernels for 0%

commit v1 on v0

v1 whole, which is shorter than its diff:
```python
import functools

import jax
import jax.numpy as jnp
from jax import lax
from jax.experimental import pallas as pl
from jax.experimental.pallas import tpu as pltpu
from jax.sharding import PartitionSpec as P

SPAN = 64
WIN = 16
PHASES = 16
MESH = pl.DeviceIdType.MESH
F32 = jnp.float32
BF16 = jnp.bfloat16


def window_sum(rows, width):
    reach = 1
    while reach < width:
        rows = rows[:-reach] + rows[reach:]
        reach *= 2
    return rows


def kernel(
    n_rx, n_ta, n_af, groups, halves,
    traces_ref, slopes_ref, offsets_ref, live_ref,
    stack_ref, coherence_ref, peak_ref,
    cols, halo, delays, long, parts, arrived, lead, lead_in, top, top_in,
    gather_send, gather_recv, halo_send, halo_recv,
    part_send, part_recv, lead_send, lead_recv, top_send, top_recv,
):
    blocks = n_ta * n_af
    members = n_rx // groups
    local_rows, block_len = traces_ref.shape
    half_rows = local_rows // halves
    group_slows = slopes_ref.shape[1] // groups
    own_slows = group_slows // members
    rx = lax.axis_index("rx")
    group, member = lax.div(rx, members), lax.rem(rx, members)
    other_rx = (groups - 1 - group) * members + member
    block = lax.axis_index("ta") * n_af + lax.axis_index("af")
    has_previous = block > 0
    has_next = block < blocks - 1

    def at_block(number):
        return {"ta": lax.div(number, n_af), "af": lax.rem(number, n_af)}

    previous = at_block(jnp.maximum(block - 1, 0))
    block_peers = [at_block(lax.rem(block + step, blocks)) for step in range(1, blocks)]
    member_peers = [lax.rem(member + step, members) for step in range(1, members)]

    peers = list(block_peers)
    peers += [{"rx": group * members + peer} for peer in member_peers]
    if groups > 1:
        peers.append({"rx": other_rx})
    barrier = pltpu.get_barrier_semaphore()
    for peer in peers:
        pl.semaphore_signal(barrier, inc=1, device_id=peer, device_id_type=MESH)

    for half in range(halves):
        rows = traces_ref[half * half_rows : (half + 1) * half_rows, :]
        cols[half] = rows.astype(F32).T.astype(BF16)

    @pl.when(jnp.logical_not(has_next))
    def _():
        halo[...] = jnp.zeros_like(halo)
        lead_in[...] = jnp.zeros_like(lead_in)

    pl.semaphore_wait(barrier, len(peers))

    def gather(half):
        return pltpu.make_async_remote_copy(
            src_ref=cols.at[half], dst_ref=cols.at[halves + half],
            send_sem=gather_send.at[half], recv_sem=gather_recv.at[half],
            device_id={"rx": other_rx}, device_id_type=MESH,
        )

    def pass_halo(index):
        return pltpu.make_async_remote_copy(
            src_ref=cols.at[index, pl.ds(0, SPAN)], dst_ref=halo.at[index],
            send_sem=halo_send.at[index], recv_sem=halo_recv.at[index],
            device_id=previous, device_id_type=MESH,
        )

    @pl.when(has_previous)
    def _():
        for half in range(halves):
            pass_halo(half).start()

    if groups > 1:
        for half in range(halves):
            gather(half).start()

    slopes = slopes_ref[:, pl.ds(pl.multiple_of(group * group_slows, group_slows), group_slows)]
    slopes = slopes.astype(F32)
    for index in range(groups * halves):
        side, half = divmod(index, halves)
        start = (other_rx if side else rx) * local_rows + half * half_rows
        lanes = pl.ds(pl.multiple_of(start, half_rows), half_rows)
        offsets = offsets_ref[:, lanes].astype(F32)
        marked = jnp.where(live_ref[:, lanes] != 0, offsets, 65536.0)
        column = jnp.broadcast_to(marked, (128, half_rows)).T
        column = jnp.concatenate([column] * (-(-group_slows // 128)), axis=1)[:, :group_slows]
        delay = jnp.floor(column * slopes * (1.0 / 65536.0))
        delays[index] = jnp.where(column < 65536.0, delay, 127.0).astype(BF16)

    parts[...] = jnp.zeros_like(parts)
    kept = block_len + SPAN - PHASES

    def add_block(index, carry):
        if groups > 1:
            @pl.when(jnp.logical_and(index >= 1, index <= halves))
            def _():
                gather(index - 1).wait_recv()

                @pl.when(has_previous)
                def _():
                    pass_halo(index - 1 + halves).start()

        @pl.when(has_next)
        def _():
            pass_halo(index).wait_recv()

        long[0:block_len] = cols[index].astype(F32)
        long[block_len:] = halo[index].astype(F32)
        delay = delays[index]
        for phase in range(PHASES):
            samples = long[phase : phase + kept]
            squares = (samples * samples).astype(BF16)
            samples = samples.astype(BF16)
            left, right = [], []
            for lag in range(0, SPAN, PHASES):
                left.append(jnp.concatenate(
                    [samples[lag : lag + block_len], squares[lag : lag + block_len]], axis=0))
                right.append(jnp.where(delay == jnp.asarray(lag + phase, BF16),
                                       jnp.asarray(1, BF16), jnp.asarray(0, BF16)))
            product = jnp.dot(jnp.concatenate(left, axis=1), jnp.concatenate(right, axis=0),
                              preferred_element_type=F32)
            for part in range(members):
                parts[part] += product[:, part * own_slows : (part + 1) * own_slows]
        return carry

    lax.fori_loop(0, groups * halves, add_block, 0)

    exchanges = []
    for step, peer in enumerate(member_peers):
        exchanges.append(pltpu.make_async_remote_copy(
            src_ref=parts.at[peer], dst_ref=arrived.at[step],
            send_sem=part_send.at[step], recv_sem=part_recv.at[step],
            device_id={"rx": group * members + peer}, device_id_type=MESH,
        ))
        exchanges[-1].start()
    total = parts[member]
    for step, exchange in enumerate(exchanges):
        exchange.wait_recv()
        total = total + arrived[step]

    stack, energy = total[:block_len], total[block_len:]
    lead[0:WIN] = stack[:WIN]
    lead[WIN:] = energy[:WIN]
    pass_lead = pltpu.make_async_remote_copy(
        src_ref=lead, dst_ref=lead_in, send_sem=lead_send, recv_sem=lead_recv,
        device_id=previous, device_id_type=MESH,
    )

    @pl.when(has_previous)
    def _():
        pass_lead.start()

    stack_ref[...] = stack.T

    @pl.when(has_next)
    def _():
        pass_lead.wait_recv()

    long_stack = jnp.concatenate([stack, lead_in[0:WIN]], axis=0)
    long_energy = jnp.concatenate([energy, lead_in[WIN:]], axis=0)
    power_sum = window_sum(long_stack * long_stack, WIN)[:block_len]
    energy_sum = window_sum(long_energy, WIN)[:block_len]
    coherence = power_sum / jnp.maximum(energy_sum, 1.0)
    peak = jnp.max(coherence, axis=0, keepdims=True)
    top[...] = peak
    tops = []
    for step, peer in enumerate(block_peers):
        tops.append(pltpu.make_async_remote_copy(
            src_ref=top, dst_ref=top_in.at[step],
            send_sem=top_send.at[step], recv_sem=top_recv.at[step],
            device_id=peer, device_id_type=MESH,
        ))
        tops[-1].start()
    coherence_ref[...] = coherence.T
    for step, copy in enumerate(tops):
        copy.wait_recv()
        peak = jnp.maximum(peak, top_in[step])
    peak_ref[...] = peak

    for copy in tops + exchanges:
        copy.wait_send()
    if groups > 1:
        for half in range(halves):
            gather(half).wait_send()

    @pl.when(has_previous)
    def _():
        pass_lead.wait_send()
        for index in range(groups * halves):
            pass_halo(index).wait_send()


def solution(mesh):
    n_rx, n_ta, n_af = (mesh.shape[name] for name in ("rx", "ta", "af"))
    groups = 2 if n_rx % 2 == 0 else 1
    members = n_rx // groups

    def on_device(traces, slopes, offsets, live):
        local_rows, block_len = traces.shape
        halves = 2 if local_rows % 512 == 0 else 1
        half_rows = local_rows // halves
        group_slows = slopes.shape[0] // groups
        own_slows = group_slows // members
        sides = groups * halves
        dma = pltpu.SemaphoreType.DMA
        blocks = n_ta * n_af
        vmem = pl.BlockSpec(memory_space=pltpu.VMEM)
        stack, coherence, peak = pl.pallas_call(
            functools.partial(kernel, n_rx, n_ta, n_af, groups, halves),
            out_shape=(
                jax.ShapeDtypeStruct((own_slows, block_len), F32),
                jax.ShapeDtypeStruct((own_slows, block_len), F32),
                jax.ShapeDtypeStruct((1, own_slows), F32),
            ),
            in_specs=[vmem] * 4,
            out_specs=(vmem,) * 3,
            scratch_shapes=[
                pltpu.VMEM((sides, block_len, half_rows), BF16),
                pltpu.VMEM((sides, SPAN, half_rows), BF16),
                pltpu.VMEM((sides, half_rows, group_slows), BF16),
                pltpu.VMEM((block_len + SPAN, half_rows), F32),
                pltpu.VMEM((members, 2 * block_len, own_slows), F32),
                pltpu.VMEM((max(members - 1, 1), 2 * block_len, own_slows), F32),
                pltpu.VMEM((2 * WIN, own_slows), F32),
                pltpu.VMEM((2 * WIN, own_slows), F32),
                pltpu.VMEM((1, own_slows), F32),
                pltpu.VMEM((max(blocks - 1, 1), 1, own_slows), F32),
                dma((halves,)), dma((halves,)),
                dma((sides,)), dma((sides,)),
                dma((max(members - 1, 1),)), dma((max(members - 1, 1),)),
                dma, dma,
                dma((max(blocks - 1, 1),)), dma((max(blocks - 1, 1),)),
            ],
            compiler_params=pltpu.CompilerParams(collective_id=0, has_side_effects=True),
            name="slant_stack",
        )(traces, slopes[None], offsets[None], live[None])
        return stack, coherence, peak[0]

    return jax.shard_map(
        on_device,
        mesh=mesh,
        in_specs=(P(("shots", "rx"), ("ta", "af")), P(), P("shots"), P("shots")),
        out_specs=(
            P(("shots", "rx"), ("ta", "af")),
            P(("shots", "rx"), ("ta", "af")),
            P(("shots", "rx")),
        ),
        check_vma=False,
    )
```

time: 148 us -> 29.6 us (0.20)
  the two profiles are of different devices: /device:TPU:0 before, /device:TPU:10 now
where the time goes in v1:
time: 29.6 us; the launch traced here: 29.4 us
  Pallas kernels  26.1 us (88%)
  local copies, waits for them, and re-layouts  2.65 us (9%)
  between operations  0.65 us (2%)
    pallas_call x1, Pallas kernels, on_device(): pl.pallas_call(functools.partial(kernel, n_rx, n_ta, n_af, groups, halves...  26.1 us
    unnamed x7, local copies, waits for them, and re-layouts  2.65 us

profile of v1, /device:TPU:10, one launch (start us, length us, event | category | flops | bytes accessed | tf_op | source)
XLA Modules:
  0.0 29.4 jit_solution(10231726153673959988)
XLA Ops:
  0.6 26.1 %slant_stack.1 = (f32[128,128]{1,0:T(8,128)}, f32[128,128]{1,0:T(8,128)}, f32[1,128]{1,0:T(1,128)}) custom-call(bf16[512,128]{1,0:T(8,128)(2,1)} %traces_ref.1, s32[1,512]{1,0:T(1,128)} %bitcast.6, s32[1,2048]{1,0:T(1,128)} %bitcast.4, s32[1,2048]{1,0:T(1,128)} %bitcast.5), custom_call_target="tpu_custom_call" | custom-call | tf_op jit(solution)/shard_map/slant_stack/pallas_call | solution.py:227
  26.7 0.0 copy-start
  26.8 1.5 %copy.10 = f32[128,128]{1,0:T(8,128)} copy(f32[128,128]{1,0:T(8,128)} %get-tuple-element.12) | data formatting | bytes 131072
  28.3 0.0 copy-done
  28.3 0.0 copy-start.1
  28.3 0.6 %copy.11 = f32[128,128]{1,0:T(8,128)} copy(f32[128,128]{1,0:T(8,128)S(1)} %copy-done) | data formatting | bytes 131072
  28.9 0.0 copy-done.1
  28.9 0.5 %copy.12 = f32[128]{0:T(128)} copy(f32[128]{0:T(128)S(1)} %bitcast.7) | data formatting | bytes 1024
Async XLA Ops:
  26.7 1.5 %copy-start = (f32[128,128]{1,0:T(8,128)S(1)}, f32[128,128]{1,0:T(8,128)}, u32[]{:S(2)}) copy-start(f32[128,128]{1,0:T(8,128)} %get-tuple-element.13) | copy-start | bytes 196612
  28.3 0.6 %copy-start.1 = (f32[1,128]{1,0:T(1,128)S(1)}, f32[1,128]{1,0:T(1,128)}, u32[]{:S(2)}) copy-start(f32[1,128]{1,0:T(1,128)} %get-tuple-element.8) | copy-start | bytes 1540

commit v2 on v1

--- a/solution.py
+++ b/solution.py
@@ -51,10 +51,12 @@
     block_peers = [at_block(lax.rem(block + step, blocks)) for step in range(1, blocks)]
     member_peers = [lax.rem(member + step, members) for step in range(1, members)]
 
-    peers = list(block_peers)
-    peers += [{"rx": group * members + peer} for peer in member_peers]
-    if groups > 1:
-        peers.append({"rx": other_rx})
+    peers = list(block_peers) + [{"rx": other_rx}]
+    for peer in member_peers:
+        peer_rx = {"rx": group * members + peer}
+        peers.append(peer_rx)
+        if blocks > 1:
+            peers += [peer_rx | block_peers[0], peer_rx | block_peers[-1]]
     barrier = pltpu.get_barrier_semaphore()
     for peer in peers:
         pl.semaphore_signal(barrier, inc=1, device_id=peer, device_id_type=MESH)
@@ -89,9 +91,8 @@
         for half in range(halves):
             pass_halo(half).start()
 
-    if groups > 1:
-        for half in range(halves):
-            gather(half).start()
+    for half in range(halves):
+        gather(half).start()
 
     slopes = slopes_ref[:, pl.ds(pl.multiple_of(group * group_slows, group_slows), group_slows)]
     slopes = slopes.astype(F32)
@@ -107,76 +108,114 @@
         delays[index] = jnp.where(column < 65536.0, delay, 127.0).astype(BF16)
 
     parts[...] = jnp.zeros_like(parts)
-    kept = block_len + SPAN - PHASES
-
-    def add_block(index, carry):
-        if groups > 1:
-            @pl.when(jnp.logical_and(index >= 1, index <= halves))
-            def _():
-                gather(index - 1).wait_recv()
-
-                @pl.when(has_previous)
-                def _():
-                    pass_halo(index - 1 + halves).start()
-
-        @pl.when(has_next)
-        def _():
-            pass_halo(index).wait_recv()
-
-        long[0:block_len] = cols[index].astype(F32)
-        long[block_len:] = halo[index].astype(F32)
+    cut = block_len // 2
+    kept = cut + SPAN - PHASES
+
+    def add_block(index, upper):
+        first = cut if upper else 0
+        long[first:block_len] = cols[index, first:].astype(F32)
+        if upper:
+            long[block_len:] = halo[index].astype(F32)
         delay = delays[index]
         for phase in range(PHASES):
-            samples = long[phase : phase + kept]
+            samples = long[first + phase : first + phase + kept]
             squares = (samples * samples).astype(BF16)
             samples = samples.astype(BF16)
             left, right = [], []
             for lag in range(0, SPAN, PHASES):
                 left.append(jnp.concatenate(
-                    [samples[lag : lag + block_len], squares[lag : lag + block_len]], axis=0))
+                    [samples[lag : lag + cut], squares[lag : lag + cut]], axis=0))
                 right.append(jnp.where(delay == jnp.asarray(lag + phase, BF16),
                                        jnp.asarray(1, BF16), jnp.asarray(0, BF16)))
             product = jnp.dot(jnp.concatenate(left, axis=1), jnp.concatenate(right, axis=0),
                               preferred_element_type=F32)
             for part in range(members):
-                parts[part] += product[:, part * own_slows : (part + 1) * own_slows]
+                parts[int(upper), part] += product[:, part * own_slows : (part + 1) * own_slows]
+
+    def wait_halo(index):
+        @pl.when(has_next)
+        def _():
+            pass_halo(index).wait_recv()
+
+    def exchange(upper, step):
+        peer = member_peers[step]
+        return pltpu.make_async_remote_copy(
+            src_ref=parts.at[upper, peer], dst_ref=arrived.at[upper, step],
+            send_sem=part_send.at[upper, step], recv_sem=part_recv.at[upper, step],
+            device_id={"rx": group * members + peer}, device_id_type=MESH,
+        )
+
+    def pass_lead(step):
+        peer = lax.rem(member + step, members)
+        return pltpu.make_async_remote_copy(
+            src_ref=lead.at[peer], dst_ref=lead_in.at[step],
+            send_sem=lead_send.at[step], recv_sem=lead_recv.at[step],
+            device_id={"rx": group * members + peer} | previous, device_id_type=MESH,
+        )
+
+    def own_lower(half, carry):
+        add_block(half, False)
         return carry
 
-    lax.fori_loop(0, groups * halves, add_block, 0)
-
-    exchanges = []
-    for step, peer in enumerate(member_peers):
-        exchanges.append(pltpu.make_async_remote_copy(
-            src_ref=parts.at[peer], dst_ref=arrived.at[step],
-            send_sem=part_send.at[step], recv_sem=part_recv.at[step],
-            device_id={"rx": group * members + peer}, device_id_type=MESH,
-        ))
-        exchanges[-1].start()
-    total = parts[member]
-    for step, exchange in enumerate(exchanges):
-        exchange.wait_recv()
-        total = total + arrived[step]
-
-    stack, energy = total[:block_len], total[block_len:]
-    lead[0:WIN] = stack[:WIN]
-    lead[WIN:] = energy[:WIN]
-    pass_lead = pltpu.make_async_remote_copy(
-        src_ref=lead, dst_ref=lead_in, send_sem=lead_send, recv_sem=lead_recv,
-        device_id=previous, device_id_type=MESH,
-    )
-
-    @pl.when(has_previous)
-    def _():
-        pass_lead.start()
-
-    stack_ref[...] = stack.T
+    def own_upper(half, carry):
+        wait_halo(half)
+        add_block(half, True)
+        return carry
+
+    def other_side(half, carry):
+        gather(half).wait_recv()
+
+        @pl.when(has_previous)
+        def _():
+            pass_halo(halves + half).start()
+
+        add_block(halves + half, False)
+
+        @pl.when(half == halves - 1)
+        def _():
+            for part in range(members):
+                lead[part, 0:WIN] = parts[0, part, 0:WIN]
+                lead[part, WIN:] = parts[0, part, cut : cut + WIN]
+
+            @pl.when(has_previous)
+            def _():
+                for step in range(members):
+                    pass_lead(step).start()
+
+            for step in range(members - 1):
+                exchange(0, step).start()
+
+        wait_halo(halves + half)
+        add_block(halves + half, True)
+        return carry
+
+    lax.fori_loop(0, halves, own_lower, 0)
+    lax.fori_loop(0, halves, own_upper, 0)
+    lax.fori_loop(0, halves, other_side, 0)
+    for step in range(members - 1):
+        exchange(1, step).start()
+
+    totals = []
+    for upper in range(2):
+        total = parts[upper, member]
+        for step in range(members - 1):
+            exchange(upper, step).wait_recv()
+            total = total + arrived[upper, step]
+        stack_ref[:, upper * cut : (upper + 1) * cut] = total[:cut].T
+        totals.append(total)
+    stack = jnp.concatenate([total[:cut] for total in totals], axis=0)
+    energy = jnp.concatenate([total[cut:] for total in totals], axis=0)
 
     @pl.when(has_next)
     def _():
-        pass_lead.wait_recv()
-
-    long_stack = jnp.concatenate([stack, lead_in[0:WIN]], axis=0)
-    long_energy = jnp.concatenate([energy, lead_in[WIN:]], axis=0)
+        for step in range(members):
+            pass_lead(step).wait_recv()
+
+    following = lead_in[0]
+    for step in range(1, members):
+        following = following + lead_in[step]
+    long_stack = jnp.concatenate([stack, following[:WIN]], axis=0)
+    long_energy = jnp.concatenate([energy, following[WIN:]], axis=0)
     power_sum = window_sum(long_stack * long_stack, WIN)[:block_len]
     energy_sum = window_sum(long_energy, WIN)[:block_len]
     coherence = power_sum / jnp.maximum(energy_sum, 1.0)
@@ -196,22 +235,25 @@
         peak = jnp.maximum(peak, top_in[step])
     peak_ref[...] = peak
 
-    for copy in tops + exchanges:
+    for copy in tops:
         copy.wait_send()
-    if groups > 1:
-        for half in range(halves):
-            gather(half).wait_send()
+    for step in range(members - 1):
+        exchange(0, step).wait_send()
+        exchange(1, step).wait_send()
+    for half in range(halves):
+        gather(half).wait_send()
 
     @pl.when(has_previous)
     def _():
-        pass_lead.wait_send()
+        for step in range(members):
+            pass_lead(step).wait_send()
         for index in range(groups * halves):
             pass_halo(index).wait_send()
 
 
 def solution(mesh):
     n_rx, n_ta, n_af = (mesh.shape[name] for name in ("rx", "ta", "af"))
-    groups = 2 if n_rx % 2 == 0 else 1
+    groups = 2
     members = n_rx // groups
 
     def on_device(traces, slopes, offsets, live):
@@ -238,16 +280,16 @@
                 pltpu.VMEM((sides, SPAN, half_rows), BF16),
                 pltpu.VMEM((sides, half_rows, group_slows), BF16),
                 pltpu.VMEM((block_len + SPAN, half_rows), F32),
-                pltpu.VMEM((members, 2 * block_len, own_slows), F32),
-                pltpu.VMEM((max(members - 1, 1), 2 * block_len, own_slows), F32),
-                pltpu.VMEM((2 * WIN, own_slows), F32),
-                pltpu.VMEM((2 * WIN, own_slows), F32),
+                pltpu.VMEM((2, members, block_len, own_slows), F32),
+                pltpu.VMEM((2, max(members - 1, 1), block_len, own_slows), F32),
+                pltpu.VMEM((members, 2 * WIN, own_slows), F32),
+                pltpu.VMEM((members, 2 * WIN, own_slows), F32),
                 pltpu.VMEM((1, own_slows), F32),
                 pltpu.VMEM((max(blocks - 1, 1), 1, own_slows), F32),
                 dma((halves,)), dma((halves,)),
                 dma((sides,)), dma((sides,)),
-                dma((max(members - 1, 1),)), dma((max(members - 1, 1),)),
-                dma, dma,
+                dma((2, max(members - 1, 1))), dma((2, max(members - 1, 1))),
+                dma((members,)), dma((members,)),
                 dma((max(blocks - 1, 1),)), dma((max(blocks - 1, 1),)),
             ],
             compiler_params=pltpu.CompilerParams(collective_id=0, has_side_effects=True),

time: 29.6 us -> 31.6 us (1.068)
  the two profiles are of different devices: /device:TPU:10 before, /device:TPU:0 now
where the time goes in v2:
time: 31.6 us; the launch traced here: 31.4 us
  Pallas kernels  28.1 us (89%)
  local copies, waits for them, and re-layouts  2.65 us (8%)
  between operations  0.65 us (2%)
    pallas_call x1, Pallas kernels, on_device(): pl.pallas_call(functools.partial(kernel, n_rx, n_ta, n_af, groups, halves...  28.1 us
    unnamed x7, local copies, waits for them, and re-layouts  2.65 us

profile of v2, /device:TPU:0, one launch (start us, length us, event | category | flops | bytes accessed | tf_op | source)
XLA Modules:
  0.0 31.4 jit_solution(14627028825905638370)
XLA Ops:
  0.6 28.1 %slant_stack.1 = (f32[128,128]{1,0:T(8,128)}, f32[128,128]{1,0:T(8,128)}, f32[1,128]{1,0:T(1,128)}) custom-call(bf16[512,128]{1,0:T(8,128)(2,1)} %traces_ref.1, s32[1,512]{1,0:T(1,128)} %bitcast.6, s32[1,2048]{1,0:T(1,128)} %bitcast.4, s32[1,2048]{1,0:T(1,128)} %bitcast.5), custom_call_target="tpu_custom_call" | custom-call | tf_op jit(solution)/shard_map/slant_stack/pallas_call | solution.py:269
  28.7 0.0 copy-start
  28.7 1.5 %copy.10 = f32[128,128]{1,0:T(8,128)} copy(f32[128,128]{1,0:T(8,128)} %get-tuple-element.12) | data formatting | bytes 131072
  30.2 0.0 copy-done
  30.2 0.0 copy-start.1
  30.2 0.6 %copy.11 = f32[128,128]{1,0:T(8,128)} copy(f32[128,128]{1,0:T(8,128)S(1)} %copy-done) | data formatting | bytes 131072
  30.9 0.0 copy-done.1
  30.9 0.5 %copy.12 = f32[128]{0:T(128)} copy(f32[128]{0:T(128)S(1)} %bitcast.7) | data formatting | bytes 1024
Async XLA Ops:
  28.7 1.5 %copy-start = (f32[128,128]{1,0:T(8,128)S(1)}, f32[128,128]{1,0:T(8,128)}, u32[]{:S(2)}) copy-start(f32[128,128]{1,0:T(8,128)} %get-tuple-element.13) | copy-start | bytes 196612
  30.2 0.6 %copy-start.1 = (f32[1,128]{1,0:T(1,128)S(1)}, f32[1,128]{1,0:T(1,128)}, u32[]{:S(2)}) copy-start(f32[1,128]{1,0:T(1,128)} %get-tuple-element.8) | copy-start | bytes 1540
